TPU v7x, 32 devices: a whole 2x2x4 slice. The times are simulated.
32 devices in a mesh: dp: 2 (over core), seq: 4 (over y, x), tensor: 4 (over z).
Axes of the slice: x: 2, y: 2, z: 4, core: 2. Of those that a mesh axis runs over, the one named last changes fastest.
Arguments:
- tokens: bfloat16 [2, 2048, 2048], P('dp', ('seq', 'tensor')), may hold values from -6 to 6
- attn_gain: float32 [2048], replicated, may hold values from 0.5 to 1.5
- w_qkv: bfloat16 [3, 2048, 2048], P(None, None, 'tensor'), may hold values from -1 to 1
- w_out: bfloat16 [2048, 2048], P('tensor'), may hold values from -0.125 to 0.125
- mlp_gain: float32 [2048], replicated, may hold values from 0.5 to 1.5
- w_up: bfloat16 [2048, 8192], P(None, 'tensor'), may hold values from -0.125 to 0.125
- w_down: bfloat16 [8192, 2048], P('tensor'), may hold values from -0.0625 to 0.0625
- pool_gain: float32 [2048], replicated, may hold values from -8 to 8
- pool_bias: float32 [2048], replicated, may hold values from 0.5 to 5
- value_weight: float32 [2048], replicated, may hold values from -6 to 6
- valid_frames: int32 [2], replicated, may hold values from 4 to 8, as said below
Outputs:
- hidden: bfloat16 [2, 2048, 2048], P('dp', ('seq', 'tensor'))
- frame_values: float32 [2, 8], P('dp', 'seq')
- advantages: float32 [2, 8], P('dp', 'seq')
Inputs may be any that keep to these rules, and one draw needn't show every extreme that they name: `valid_frames`: at least one rollout keeps all 8 frames and at least one keeps 8 // 2 of them.
All inputs are finite; a program needn't handle non-finite values.
Results may differ from a plain program's by a relative error of at most 0.017.
Values may be sent and summed in bfloat16 or wider, within the bound.
A program may use at most 256 MiB of HBM per device.

v0:
```python
import jax
import jax.numpy as jnp
from jax import lax
from jax.sharding import PartitionSpec as P

HEAD_DIM = 128
TOK_FRAME = 256
FR_DEV = 2


def entering_2(value, axis, join, neutral):
    count, mine = (lax.axis_size(axis), lax.axis_index(axis))
    pieces = jax.tree.map(lambda part: lax.all_gather(part, axis), value)
    subtotal = jax.tree.map(
        lambda part, zero: jnp.full_like(part, 0) + jnp.asarray(zero, part.dtype), value, neutral
    )

    def turn(position, subtotal):
        longer = join(subtotal, jax.tree.map(lambda part: part[position], pieces))
        return jax.tree.map(lambda new, old: jnp.where(position < mine, new, old), longer, subtotal)

    return lax.fori_loop(0, count - 1, turn, subtotal)


def rms_norm(values, gain):
    floats = values.astype(jnp.float32)
    square = jnp.mean(floats * floats, axis=-1, keepdims=True)
    return (floats * lax.rsqrt(square + 1e-05) * gain).astype(jnp.bfloat16)


def compose(earlier, later):
    return (earlier[0] * later[0], later[0] * earlier[1] + later[1])


def local(
    tokens,
    attn_gain,
    w_qkv,
    w_out,
    mlp_gain,
    w_up,
    w_down,
    pool_gain,
    pool_bias,
    value_weight,
    valid_frames,
):
    rows = tokens[0]
    row_count = rows.shape[0]
    seq_index = lax.axis_index("seq")
    tensor_index = lax.axis_index("tensor")
    roll_index = lax.axis_index("dp")
    length = valid_frames[roll_index]
    local_heads = w_qkv.shape[2] // HEAD_DIM
    scale = 1.0 / HEAD_DIM**0.5
    block_tokens = lax.all_gather(rows, "tensor", axis=0, tiled=True)
    qkv = jnp.einsum(
        "nd,cde->nce", rms_norm(block_tokens, attn_gain), w_qkv, preferred_element_type=jnp.float32
    ).astype(jnp.bfloat16)
    block = qkv.shape[0]
    query = qkv[:, 0].reshape(block, local_heads, HEAD_DIM)
    query_frame = (seq_index * block + jnp.arange(block, dtype=jnp.int32)) // TOK_FRAME
    peak = jnp.full((local_heads, block), -1e30, jnp.float32)
    key_piece = lax.all_gather(qkv[:, 1], "seq", axis=0, tiled=True)
    value_piece = lax.all_gather(qkv[:, 2], "seq", axis=0, tiled=True)
    width = key_piece.shape[0]
    key_heads = key_piece.reshape(width, local_heads, HEAD_DIM)
    value_heads = value_piece.reshape(width, local_heads, HEAD_DIM)
    scores = (
        jnp.einsum("qhe,khe->hqk", query, key_heads, preferred_element_type=jnp.float32) * scale
    )
    key_frame = jnp.arange(width, dtype=jnp.int32) // TOK_FRAME
    allowed = (key_frame[None, :] <= query_frame[:, None]) & (key_frame[None, :] < length)
    scores = jnp.where(allowed[None], scores, -1e30)
    new_peak = jnp.maximum(peak, jnp.max(scores, axis=-1))
    weights = jnp.where(allowed[None], jnp.exp(scores - new_peak[..., None]), 0.0)
    total = jnp.sum(weights, axis=-1)
    acc = jnp.einsum(
        "hqk,khe->hqe",
        weights.astype(jnp.bfloat16),
        value_heads,
        preferred_element_type=jnp.float32,
    )
    peak, total, acc = (new_peak, total, acc)
    mixed = (
        (acc / total[..., None])
        .transpose(1, 0, 2)
        .reshape(block, local_heads * HEAD_DIM)
        .astype(jnp.bfloat16)
    )
    attn_sum = lax.psum(
        jnp.dot(mixed, w_out, preferred_element_type=jnp.float32).astype(jnp.bfloat16), "tensor"
    ).astype(jnp.float32)
    after_attn = (block_tokens.astype(jnp.float32) + attn_sum).astype(jnp.bfloat16)
    up = jax.nn.gelu(
        jnp.dot(rms_norm(after_attn, mlp_gain), w_up, preferred_element_type=jnp.float32),
        approximate=True,
    ).astype(jnp.bfloat16)
    own_after = lax.dynamic_slice_in_dim(after_attn, tensor_index * row_count, row_count, 0)
    down_sum = lax.psum_scatter(
        jnp.dot(up, w_down, preferred_element_type=jnp.float32).astype(jnp.bfloat16),
        "tensor",
        scatter_dimension=0,
        tiled=True,
    ).astype(jnp.float32)
    hidden = (own_after.astype(jnp.float32) + down_sum).astype(jnp.bfloat16)
    local_frame = (tensor_index * row_count + jnp.arange(row_count, dtype=jnp.int32)) // TOK_FRAME
    selector = (local_frame[None, :] == jnp.arange(FR_DEV, dtype=jnp.int32)[:, None]).astype(
        jnp.bfloat16
    )
    sums = jnp.dot(selector, hidden, preferred_element_type=jnp.float32)
    sums = lax.psum(sums, "tensor")
    gain, offset, head_weight = (pool_gain, pool_bias, value_weight)
    means = sums / TOK_FRAME
    frame_global = seq_index * FR_DEV + jnp.arange(FR_DEV, dtype=jnp.int32)
    valid = frame_global < length
    gate = jax.nn.sigmoid(means * gain + offset)
    decay = jnp.where(valid[:, None], gate, 1.0)
    source = jnp.where(valid[:, None], (1.0 - gate) * means, 0.0)
    agg_decay = jnp.ones_like(means[0])
    agg_source = jnp.zeros_like(means[0])
    for frame in range(FR_DEV):
        agg_decay, agg_source = compose((agg_decay, agg_source), (decay[frame], source[frame]))
    entering = entering_2(
        (agg_decay, agg_source),
        "seq",
        compose,
        (jnp.ones_like(agg_decay), jnp.zeros_like(agg_source)),
    )
    state = entering[1]
    collected = []
    for frame in range(FR_DEV):
        state = decay[frame] * state + source[frame]
        collected.append(jnp.sum(state * head_weight))
    partial_values = jnp.stack(collected)
    values = jnp.where(valid, partial_values, 0.0)
    pick = jnp.sum(jnp.where(frame_global == length - 1, values, 0.0))
    count = jnp.sum(valid_frames).astype(jnp.float32)
    slot = (jnp.arange(lax.axis_size("dp"), dtype=jnp.int32) == roll_index).astype(jnp.float32)
    entries = jnp.stack([pick, jnp.sum(values), jnp.sum(values * values)])
    table = lax.psum(entries[:, None] * slot[None, :], ("dp", "seq"))
    finals, first_sums, second_sums = (table[0], table[1], table[2])
    lengths = valid_frames.astype(jnp.float32)
    mean = jnp.sum(lengths * finals - first_sums) / count
    squares = jnp.sum(lengths * finals * finals - 2.0 * finals * first_sums + second_sums) / count
    variance = squares - mean * mean
    final = jnp.sum(finals * slot)
    gap = jnp.where(valid, final - values, 0.0)
    centered = jnp.where(valid, gap - mean, 0.0)
    advantages = jnp.where(valid, centered * lax.rsqrt(variance + 1e-05), 0.0)
    return (hidden[None], values[None], advantages[None])


def solution(mesh):
    in_specs = (
        P("dp", ("seq", "tensor"), None),
        P(),
        P(None, None, "tensor"),
        P("tensor", None),
        P(),
        P(None, "tensor"),
        P("tensor", None),
        P(),
        P(),
        P(),
        P(),
    )
    out_specs = (P("dp", ("seq", "tensor"), None), P("dp", "seq"), P("dp", "seq"))
    return jax.shard_map(local, mesh=mesh, in_specs=in_specs, out_specs=out_specs, check_vma=False)
```

profile of v0, /device:TPU:0, one launch (start us, length us, event | category | flops | bytes accessed | tf_op | source)
XLA Modules:
  0.0 369.1 jit_solution(14914907635023550377)
XLA Ops:
  7.2 0.0 copy-start
  7.2 0.0 all-gather.9.cloned.1.call-start
  7.2 0.7 all-gather.9.cloned.1.call-update
  7.9 0.0 all-gather.11.cloned.1.call-start
  8.0 50.0 %all-gather.9.cloned.1.call-done = bf16[1,512,2048]{2,1,0:T(8,128)(2,1)} async-done(((bf16[1,128,2048]{2,1,0:T(8,128)(2,1)}), bf16[1,512,2048]{2,1,0:T(8,128)(2,1)}) %all-gather.9.cloned.1.call-update) | async-done | bytes 2097168 | tf_op jit(solution)/shard_map/all_gather | solution.py:56
  58.0 2.1 fusion.17
  60.1 0.0 copy-start.5
  60.1 7.1 %fusion.36 = bf16[512,3,512]{0,2,1:T(8,128)(2,1)S(1)} fusion(bf16[3,2048,512]{2,1,0:T(8,128)(2,1)} %param.15, bf16[1,512,2048]{2,1,0:T(8,128)(2,1)} %all-gather.9.cloned.1.call-done, f32[2048]{0:T(1024)} %param.14, f32[512]{0:T(512)S(1)} %add_rsqrt_fusion.1), kind=kOutput, calls=%fused_computation.46 | convolution fusion | flops 3226206208 | bytes 9971712 | tf_op jit(solution)/shard_map/nd,cde->nce/dot_general | solution.py:57
  67.2 1.2 fusion.70
  68.3 0.0 all-gather.11.cloned.1.call-update
  68.4 0.0 all-gather.13.cloned.1.call-start
  68.4 0.7 dynamic_slice.20
  69.1 0.0 all-gather.13.cloned.1.call-update
  69.1 0.2 all-reduce.2.cloned.1.call-start
  69.3 0.6 broadcast_compare_fusion
  70.0 0.7 compare_and_fusion
  70.8 31.6 %all-gather.11.cloned.1.call-done = bf16[2048,1,512]{0,2,1:T(8,128)(2,1)} async-done(((bf16[512,1,512]{0,2,1:T(8,128)(2,1)}), bf16[2048,1,512]{0,2,1:T(8,128)(2,1)}) %all-gather.11.cloned.1.call-update) | async-done | bytes 2097168 | tf_op jit(solution)/shard_map/all_gather | solution.py:64
  102.4 5.2 %fusion = (f32[4,512]{1,0:T(4,128)S(1)}, f32[4,512,2048]{2,1,0:T(8,128)S(1)}) fusion(pred[512,2048]{1,0:T(8,128)(4,1)S(1)} %compare_and_fusion, bf16[512,4,128]{0,2,1:T(8,128)(2,1)} %bitcast.94, bf16[2048,4,128]{0,2,1:T(8,128)(2,1)} %bitcast.93), kind=kOutput, calls=%fused_computation.5 | convolution fusion | flops 1086322688 | bytes 20455424 | tf_op jit(solution)/shard_map/qhe,khe->hqk/dot_general | solution.py:70
  107.6 6.1 %copy-done.1 = f32[4,512,2048]{2,1,0:T(8,128)} copy-done((f32[4,512,2048]{2,1,0:T(8,128)}, f32[4,512,2048]{2,1,0:T(8,128)S(1)}, u32[]{:S(2)}) %copy-start.1) | copy-done | bytes 16777240
  113.7 5.0 %fusion.1 = f32[4,512]{1,0:T(4,128)S(1)} fusion(f32[4,512,2048]{2,1,0:T(8,128)S(1)} %get-tuple-element.152, f32[4,512]{1,0:T(4,128)S(1)} %broadcast_maximum_fusion, pred[512,2048]{1,0:T(8,128)(4,1)S(1)} %compare_and_fusion), kind=kLoop, calls=%fused_computation.6 | loop fusion | flops 20969472 | bytes 17842176 | tf_op jit(solution)/shard_map/reduce_sum | solution.py:77
  118.7 20.5 %all-gather.13.cloned.1.call-done = bf16[2048,1,512]{0,2,1:T(8,128)(2,1)} async-done(((bf16[512,1,512]{0,2,1:T(8,128)(2,1)}), bf16[2048,1,512]{0,2,1:T(8,128)(2,1)}) %all-gather.13.cloned.1.call-update) | async-done | bytes 2097168 | tf_op jit(solution)/shard_map/all_gather | solution.py:65
  139.3 8.7 %divide_convert_fusion = bf16[512,4,128]{0,2,1:T(8,128)(2,1)S(1)} fusion(bf16[2048,4,128]{0,2,1:T(8,128)(2,1)} %bitcast.104, f32[4,512,2048]{2,1,0:T(8,128)} %copy-done.1, f32[4,512]{1,0:T(4,128)S(1)} %broadcast_maximum_fusion, pred[512,2048]{1,0:T(8,128)(4,1)S(1)} %compare_and_fusion, f32[512,4]{0,1:T(4,128)S(1)} %bitcast.103), kind=kOutput, calls=%fused_computation.49 | convolution fusion | flops 1095237632 | bytes 20463616 | tf_op jit(solution)/shard_map/hqk,khe->hqe/dot_general | solution.py:78
  148.0 2.6 convolution_convert_fusion.1
  150.7 0.0 all-reduce.2.cloned.1.call-update
  150.7 0.3 reduce-scatter.2.cloned.1.call-start
  151.0 86.0 %all-reduce.2.cloned.1.call-done = bf16[512,2048]{1,0:T(8,128)(2,1)} async-done(((bf16[512,2048]{1,0:T(8,128)(2,1)}), bf16[512,2048]{1,0:T(8,128)(2,1)}) %all-reduce.2.cloned.1.call-update) | async-done | bytes 2097168 | tf_op jit(solution)/shard_map/psum | solution.py:91
  237.0 4.5 %fusion.6 = (f32[512]{0:T(512)S(1)}, bf16[512,2048]{1,0:T(8,128)(2,1)}) fusion(bf16[512,2048]{1,0:T(8,128)(2,1)} %all-reduce.2.cloned.1.call-done, bf16[1,512,2048]{2,1,0:T(8,128)(2,1)} %all-gather.9.cloned.1.call-done), kind=kLoop, calls=%fused_computation.16 | loop fusion | flops 7339520 | bytes 6293504 | tf_op jit(solution)/shard_map/reduce_sum | solution.py:27
  241.6 0.0 copy-start.4
  241.6 16.6 %convolution_convert_fusion = bf16[512,2048]{1,0:T(8,128)(2,1)} fusion(bf16[2048,2048]{1,0:T(8,128)(2,1)} %param.19, bf16[2048,2048]{1,0:T(8,128)(2,1)} %param.18, bf16[512,2048]{1,0:T(8,128)(2,1)} %get-tuple-element.139, f32[2048]{0:T(1024)S(1)} %copy-done.6, f32[512]{0:T(512)S(1)} %add_rsqrt_fusion), kind=kOutput, calls=%fused_computation.32 | convolution fusion | flops 8604614656 | bytes 20981760 | tf_op jit(solution)/shard_map/dot_general | solution.py:101
  258.2 0.0 reduce-scatter.2.cloned.1.call-update
  258.2 0.6 reduce_sum.118
  259.5 0.6 fusion.60
  260.1 40.9 %reduce-scatter.2.cloned.1.call-done = bf16[128,2048]{1,0:T(8,128)(2,1)} async-done(((bf16[512,2048]{1,0:T(8,128)(2,1)}), bf16[128,2048]{1,0:T(8,128)(2,1)}) %reduce-scatter.2.cloned.1.call-update) | async-done | bytes 524304 | tf_op jit(solution)/shard_map/reduce_scatter | solution.py:100
  301.0 1.4 fusion.44
  302.4 17.2 %psum.22 = f32[2,2048]{1,0:T(2,128)S(1)} all-reduce(f32[2,2048]{1,0:T(2,128)S(1)} %fusion.44), channel_id=1, replica_groups=mesh['dp'=2,'seq'=4,'tensor'=4] {'tensor'}, use_global_device_ids=true, to_apply=%region_6.7 | all-reduce | flops 4096 | bytes 32768 | tf_op jit(solution)/shard_map/psum | solution.py:112
  319.6 0.1 broadcast_select_fusion
  319.7 0.1 multiply_select_fusion.1
  319.8 7.9 %all-gather.4 = f32[4,1,2048]{2,1,0:T(1,128)S(1)} all-gather(f32[1,1,2048]{2,1,0:T(1,128)S(1)} %get-tuple-element.147), channel_id=1, replica_groups=mesh['dp'=2,'seq'=4,'tensor'=4] {'seq'}, dimensions={0}, use_global_device_ids=true | all-gather | bytes 40960 | tf_op jit(solution)/shard_map/all_gather | solution.py:13
  327.8 8.1 %all-gather.3 = f32[4,1,2048]{2,1,0:T(1,128)S(1)} all-gather(f32[1,1,2048]{2,1,0:T(1,128)S(1)} %get-tuple-element.146), channel_id=1, replica_groups=mesh['dp'=2,'seq'=4,'tensor'=4] {'seq'}, dimensions={0}, use_global_device_ids=true | all-gather | bytes 40960 | tf_op jit(solution)/shard_map/all_gather | solution.py:13
  335.9 0.2 while.14
  336.1 0.6 multiply_reduce_fusion.1
  336.7 2.6 fusion.55
  339.3 2.0 pad_maximum_fusion
  341.3 0.1 broadcast_multiply_fusion.1
  341.9 13.4 %psum.23 = f32[3,2]{1,0:T(4,128)S(1)} all-reduce(f32[3,2]{1,0:T(4,128)S(1)} %broadcast_multiply_fusion.1), channel_id=1, replica_groups=mesh['dp'=2,'seq'=4,'tensor'=4] {'dp','seq'}, use_global_device_ids=true, to_apply=%region_14.15 | all-reduce | flops 6 | bytes 48 | tf_op jit(solution)/shard_map/psum | solution.py:141
  355.3 0.6 fusion.57
  357.3 3.1 multiply_select_fusion.2
  360.4 2.1 fusion.45
  (28 shorter events, 0.2 us)
Async XLA Ops:
  7.2 140.9 %copy-start = (bf16[512,2048]{1,0:T(8,128)(2,1)S(1)}, bf16[512,2048]{1,0:T(8,128)(2,1)}, u32[]{:S(2)}) copy-start(bf16[512,2048]{1,0:T(8,128)(2,1)} %param.16) | copy-start | bytes 6291460
  7.2 50.8 %all-gather.9.cloned.1.call-start = ((), (), s32[]{:S(2)}) async-start(), calls=%async_computation.3 | async-start | bytes 2621440 | tf_op jit(solution)/shard_map/all_gather | solution.py:56
  7.9 94.5 %all-gather.11.cloned.1.call-start = ((), (), s32[]{:S(2)}) async-start(), calls=%async_computation.4 | async-start | bytes 2621440 | tf_op jit(solution)/shard_map/all_gather | solution.py:64
  60.1 8.4 %copy-start.5 = (s32[2]{0:T(128)S(1)}, s32[2]{0:T(128)}, u32[]{:S(2)}) copy-start(s32[2]{0:T(128)} %param.23) | copy-start | bytes 28
  68.4 70.9 %all-gather.13.cloned.1.call-start = ((), (), s32[]{:S(2)}) async-start(), calls=%async_computation.5 | async-start | bytes 2621440 | tf_op jit(solution)/shard_map/all_gather | solution.py:65
  69.1 167.9 %all-reduce.2.cloned.1.call-start = ((), (), s32[]{:S(2)}) async-start(), calls=%async_computation.1 | async-start | bytes 4194304 | tf_op jit(solution)/shard_map/psum | solution.py:91
  107.6 6.1 %copy-start.1 = (f32[4,512,2048]{2,1,0:T(8,128)}, f32[4,512,2048]{2,1,0:T(8,128)S(1)}, u32[]{:S(2)}) copy-start(f32[4,512,2048]{2,1,0:T(8,128)S(1)} %get-tuple-element.152) | copy-start | bytes 50331652
  150.7 90.9 %copy-start.6 = (f32[2048]{0:T(1024)S(1)}, f32[2048]{0:T(1024)}, u32[]{:S(2)}) copy-start(f32[2048]{0:T(1024)} %param.17) | copy-start | bytes 24580
  150.7 150.3 %reduce-scatter.2.cloned.1.call-start = ((), (), s32[]{:S(2)}) async-start(), calls=%async_computation.2 | async-start | bytes 2621440 | tf_op jit(solution)/shard_map/reduce_scatter | solution.py:100
  241.6 18.6 %copy-start.3 = (f32[2048]{0:T(1024)S(1)}, f32[2048]{0:T(1024)}, u32[]{:S(2)}) copy-start(f32[2048]{0:T(1024)} %param.20) | copy-start | bytes 24580
  241.6 78.0 %copy-start.4 = (f32[2048]{0:T(1024)S(1)}, f32[2048]{0:T(1024)}, u32[]{:S(2)}) copy-start(f32[2048]{0:T(1024)} %param.21) | copy-start | bytes 24580
  258.2 77.9 %copy-start.2 = (f32[2048]{0:T(1024)S(1)}, f32[2048]{0:T(1024)}, u32[]{:S(2)}) copy-start(f32[2048]{0:T(1024)} %param.22) | copy-start | bytes 24580
Sparse Core Ops, SparseCore 0:
  9.6 48.3 all-gather.8
  68.5 33.8 all-gather.10
  104.2 35.0 all-gather.12
  150.8 86.1 all-reduce.1
  258.3 42.6 reduce-scatter.1
where the time goes:
time: 370 us; the launch traced here: 369 us
  waiting for transfers between devices  230 us (62%)
  blocking collectives  46.6 us (13%)
  matrix products  41.7 us (11%)
  other arithmetic  25.7 us (7%)
  between operations  16.5 us (4%)
  local copies, waits for them, and re-layouts  8.01 us (2%)
    psum x1, waiting for transfers between devices, local(): lax.psum(jnp.dot(mixed, w_out, preferred_element_type=jnp.float32).astype...  86 us
    all_gather x1, waiting for transfers between devices, local(): block_tokens = lax.all_gather(rows, 'tensor', axis=0, tiled=True)  50 us
    reduce_scatter x1, waiting for transfers between devices, local(): lax.psum_scatter(jnp.dot(up, w_down, preferred_element_type=jnp.float32)....  40.9 us
    all_gather x1, waiting for transfers between devices, local(): key_piece = lax.all_gather(qkv[:, 1], 'seq', axis=0, tiled=True)  31.6 us
    all_gather x1, waiting for transfers between devices, local(): value_piece = lax.all_gather(qkv[:, 2], 'seq', axis=0, tiled=True)  20.5 us
    psum x1, blocking collectives, local(): sums = lax.psum(sums, 'tensor')  17.2 us
    dot_general x1, matrix products, local(): jnp.dot(up, w_down, preferred_element_type=jnp.float32).astype(jnp.bfloat16)  16.6 us
    all_gather x2, blocking collectives, entering_2(): pieces = jax.tree.map(lambda part: lax.all_gather(part, axis), value)  16 us
  transfers between devices with their start and end apart: 5, of which 5 were waited for; matrix products, arithmetic and copies ran while one was open for 4% of the time, Pallas kernels for 0%

commit v1 on v0

v1 whole, which is shorter than its diff:
```python
import functools

import jax
import jax.numpy as jnp
from jax import lax
from jax.experimental import pallas as pl
from jax.experimental.pallas import tpu as pltpu
from jax.sharding import PartitionSpec as P

HEAD_DIM = 128
TOK_FRAME = 256
LANES = 128
MESH = pl.DeviceIdType.MESH
F32 = jnp.float32
BF16 = jnp.bfloat16


def rms_norm(floats, gain):
    square = jnp.mean(floats * floats, axis=-1, keepdims=True)
    return (floats * lax.rsqrt(square + 1e-05) * gain).astype(BF16)


def kernel(
    tok, attn_gain, w_qkv_h, w_out_h, mlp_gain, w_up_h, w_down_h, pool_gain, pool_bias,
    value_weight, lens,
    hidden, small,
    w_qkv, w_out, w_up, w_down, ag1, ag2, query, kv, peak, total, acc, mixed, part, rs,
    after, upbuf, fsum, means,
    wsem, ag_s, ag_r, kv_s, kv_r, rs_s, rs_r, fs_s, fs_r, mn_s, mn_r,
):
    T, S, DP = (lax.axis_size("tensor"), lax.axis_size("seq"), lax.axis_size("dp"))
    z, me, roll = (lax.axis_index("tensor"), lax.axis_index("seq"), lax.axis_index("dp"))
    rows, width = tok.shape
    block = rows * T
    heads = query.shape[-1] // HEAD_DIM
    hcols = query.shape[-1]
    ff = w_up.shape[1]
    fr_dev = block // TOK_FRAME
    scale = 1.0 / HEAD_DIM**0.5
    right, left = (lax.rem(z + 1, T), lax.rem(z + T - 1, T))
    tile = 512

    loads = [
        pltpu.make_async_copy(src, dst, wsem.at[i])
        for i, (src, dst) in enumerate(
            ((w_qkv_h, w_qkv), (w_out_h, w_out), (w_up_h, w_up), (w_down_h, w_down))
        )
    ]
    for load in loads:
        load.start()

    barrier = pltpu.get_barrier_semaphore()
    for d in range(1, T):
        pl.semaphore_signal(barrier, 1, device_id={"tensor": lax.rem(z + d, T)}, device_id_type=MESH)
    peers = []
    for a in range(DP):
        for b in range(S):
            if a or b:
                peers.append({"dp": lax.rem(roll + a, DP), "seq": lax.rem(me + b, S)})
    for peer in peers:
        pl.semaphore_signal(barrier, 1, device_id=peer, device_id_type=MESH)

    ag1[z] = rms_norm(tok[...].astype(F32), attn_gain[...])
    pl.semaphore_wait(barrier, T - 1 + len(peers))

    def zcopy(src, dst, s_sem, r_sem, to):
        return pltpu.make_async_remote_copy(
            src_ref=src, dst_ref=dst, send_sem=s_sem, recv_sem=r_sem,
            device_id={"tensor": to}, device_id_type=MESH,
        )

    def gather(buf, which, process):
        def send(s, way):
            return zcopy(
                buf.at[s], buf.at[s], ag_s.at[which, way, s], ag_r.at[which, s],
                right if way == 0 else left,
            )

        @pl.when(z < T - 1)
        def _():
            send(z, 0).start()

        @pl.when(z > 0)
        def _():
            send(z, 1).start()

        process(z)

        def step(k, carry):
            a, b = (z - k, z + k)

            @pl.when(a >= 0)
            def _():
                send(a, 0).wait_recv()

                @pl.when(z < T - 1)
                def _():
                    send(a, 0).start()

            @pl.when(b < T)
            def _():
                send(b, 1).wait_recv()

                @pl.when(z > 0)
                def _():
                    send(b, 1).start()

            @pl.when(a >= 0)
            def _():
                process(a)

            @pl.when(b < T)
            def _():
                process(b)

            return carry

        lax.fori_loop(1, T, step, 0)

        for s in range(T):

            @pl.when((s <= z) & (z < T - 1))
            def _():
                send(s, 0).wait_send()

            @pl.when((s >= z) & (z > 0))
            def _():
                send(s, 1).wait_send()

    def scatter(buf, which):
        def send(d, way):
            return zcopy(
                buf.at[way, d], buf.at[way, d], rs_s.at[which, way, d], rs_r.at[which, way, d],
                right if way == 0 else left,
            )

        def hop(d, way, first):
            @pl.when(first)
            def _():
                buf[way, d] = part[d]

            @pl.when(jnp.logical_not(first))
            def _():
                send(d, way).wait_recv()
                buf[way, d] = (buf[way, d].astype(F32) + part[d].astype(F32)).astype(BF16)

            send(d, way).start()

        for k in range(T - 1):
            d = T - 1 - k

            @pl.when(z < d)
            def _(d=d):
                hop(d, 0, z == 0)

            @pl.when(z > k)
            def _(d=k):
                hop(d, 1, z == T - 1)

        after[...] = after[...] + part[z].astype(F32)

        @pl.when(z > 0)
        def _():
            send(z, 0).wait_recv()
            after[...] = after[...] + buf[0, z].astype(F32)

        @pl.when(z < T - 1)
        def _():
            send(z, 1).wait_recv()
            after[...] = after[...] + buf[1, z].astype(F32)

        for d in range(T):

            @pl.when(z < d)
            def _(d=d):
                send(d, 0).wait_send()

            @pl.when(z > d)
            def _(d=d):
                send(d, 1).wait_send()

    def kv_send(d, s):
        return pltpu.make_async_remote_copy(
            src_ref=kv.at[me, s], dst_ref=kv.at[me, s], send_sem=kv_s.at[d, s],
            recv_sem=kv_r.at[me, s], device_id={"seq": lax.rem(me + d, S)}, device_id_type=MESH,
        )

    def project(s):
        x = ag1[s]
        kv[me, s, 0] = jnp.dot(x, w_qkv[1], preferred_element_type=F32).astype(BF16)
        kv[me, s, 1] = jnp.dot(x, w_qkv[2], preferred_element_type=F32).astype(BF16)
        for d in range(1, S):

            @pl.when(me + d < S)
            def _(d=d):
                kv_send(d, s).start()

        query[s] = jnp.dot(x, w_qkv[0], preferred_element_type=F32).astype(BF16)

    loads[0].wait()
    gather(ag1, 0, project)

    peak[...] = jnp.full_like(peak, -1e30)
    total[...] = jnp.zeros_like(total)
    acc[...] = jnp.zeros_like(acc)
    length = lens[pl.ds(roll, 1)][0, 0:1, 0:1].astype(jnp.int32)

    def attend(j):
        q_frame = me * fr_dev + lax.broadcasted_iota(jnp.int32, (block, 1), 0) // TOK_FRAME
        k_frame = j * fr_dev + lax.broadcasted_iota(jnp.int32, (1, block), 1) // TOK_FRAME
        allowed = (k_frame <= q_frame) & (k_frame < length)

        def head(h, carry):
            cols = pl.ds(pl.multiple_of(h * HEAD_DIM, HEAD_DIM), HEAD_DIM)
            q = query[:, :, cols].reshape(block, HEAD_DIM)
            k = kv[j, :, 0, :, cols].reshape(block, HEAD_DIM)
            v = kv[j, :, 1, :, cols].reshape(block, HEAD_DIM)
            scores = lax.dot_general(q, k, (((1,), (1,)), ((), ())), preferred_element_type=F32)
            scores = jnp.where(allowed, scores * scale, -1e30)
            old = peak[h]
            new = jnp.maximum(old, jnp.max(scores, axis=-1, keepdims=True))
            weights = jnp.where(allowed, jnp.exp(scores - new), 0.0)
            shrink = jnp.exp(old - new)
            peak[h] = new
            total[h] = total[h] * shrink + jnp.sum(weights, axis=-1, keepdims=True)
            acc[h] = acc[h] * shrink + jnp.dot(weights.astype(BF16), v, preferred_element_type=F32)
            return carry

        lax.fori_loop(0, heads, head, 0)

    attend(me)

    def earlier(d, carry):
        j = me - d

        @pl.when(j >= 0)
        def _():
            for s in range(T):
                pltpu.make_async_remote_copy(
                    src_ref=kv.at[j, s], dst_ref=kv.at[j, s], send_sem=kv_s.at[0, s],
                    recv_sem=kv_r.at[j, s], device_id={"seq": lax.rem(me + 1, S)},
                    device_id_type=MESH,
                ).wait_recv()
            attend(j)

        return carry

    lax.fori_loop(1, S, earlier, 0)
    for h in range(heads):
        mixed[:, h * HEAD_DIM : (h + 1) * HEAD_DIM] = (acc[h] / total[h]).astype(BF16)

    loads[1].wait()

    def out_tile(n, carry):
        cols = pl.ds(pl.multiple_of(n * tile, tile), tile)
        res = jnp.dot(mixed[...], w_out[:, cols], preferred_element_type=F32)
        part[:, :, cols] = res.astype(BF16).reshape(T, rows, tile)
        return carry

    lax.fori_loop(0, width // tile, out_tile, 0)
    after[...] = tok[...].astype(F32)
    scatter(rs, 0)
    rounded = after[...].astype(BF16).astype(F32)
    after[...] = rounded
    ag2[z] = rms_norm(rounded, mlp_gain[...])
    loads[2].wait()
    loads[3].wait()

    def feed(s):
        def up_tile(n, carry):
            cols = pl.ds(pl.multiple_of(n * tile, tile), tile)
            res = jnp.dot(ag2[s], w_up[:, cols], preferred_element_type=F32)
            upbuf[:, cols] = jax.nn.gelu(res, approximate=True).astype(BF16)
            return carry

        lax.fori_loop(0, ff // tile, up_tile, 0)

        def down_tile(n, carry):
            cols = pl.ds(pl.multiple_of(n * tile, tile), tile)
            res = jnp.dot(upbuf[...], w_down[:, cols], preferred_element_type=F32)
            part[s, :, cols] = res.astype(BF16)
            return carry

        lax.fori_loop(0, width // tile, down_tile, 0)

    gather(ag2, 1, feed)
    scatter(rs, 1)
    out = after[...].astype(BF16)
    hidden[...] = out
    sums = jnp.sum(out.astype(F32), axis=0, keepdims=True)
    chunks = width // LANES
    for c in range(chunks):
        fsum[z, c : c + 1, :] = sums[:, c * LANES : (c + 1) * LANES]

    def fs_send(d):
        return zcopy(fsum.at[z], fsum.at[z], fs_s.at[d], fs_r.at[z], lax.rem(z + d, T))

    for d in range(1, T):
        fs_send(d).start()
    for d in range(1, T):
        o = lax.rem(z + T - d, T)
        zcopy(fsum.at[o], fsum.at[o], fs_s.at[0], fs_r.at[o], right).wait_recv()
    per = T // fr_dev
    for f in range(fr_dev):
        m = fsum[f * per]
        for s in range(f * per + 1, (f + 1) * per):
            m = m + fsum[s]
        means[roll, me, f] = m / TOK_FRAME

    def mn_send(i, peer):
        return pltpu.make_async_remote_copy(
            src_ref=means.at[roll, me], dst_ref=means.at[roll, me], send_sem=mn_s.at[i],
            recv_sem=mn_r.at[roll, me], device_id=peer, device_id_type=MESH,
        )

    for i, peer in enumerate(peers):
        mn_send(i, peer).start()
    for a in range(DP):
        for b in range(S):
            if a or b:
                ra, sb = (lax.rem(roll + a, DP), lax.rem(me + b, S))
                pltpu.make_async_remote_copy(
                    src_ref=means.at[ra, sb], dst_ref=means.at[ra, sb], send_sem=mn_s.at[0],
                    recv_sem=mn_r.at[ra, sb], device_id=peers[0], device_id_type=MESH,
                ).wait_recv()

    lane = lax.broadcasted_iota(jnp.int32, (1, LANES), 1)
    values, gaps, valids = ([], [], [])
    for r in range(DP):
        span = lens[r]

        def frame(f, carry):
            state, vec = carry
            m = means[r, f // fr_dev, lax.rem(f, fr_dev)]
            gate = jax.nn.sigmoid(m * pool_gain[...] + pool_bias[...])
            new = gate * state + (1.0 - gate) * m
            state = jnp.where(span > f.astype(F32), new, state)
            dot = jnp.sum(jnp.sum(state * value_weight[...], axis=1, keepdims=True), axis=0, keepdims=True)
            return (state, jnp.where(lane == f, dot, vec))

        zero = (jnp.zeros((chunks, LANES), F32), jnp.zeros((1, LANES), F32))
        _, vec = lax.fori_loop(0, S * fr_dev, frame, zero)
        length_r = span[0:1].astype(jnp.int32)
        ok = lane < length_r
        vec = jnp.where(ok, vec, 0.0)
        reward = jnp.sum(jnp.where(lane == length_r - 1, vec, 0.0), axis=1, keepdims=True)
        values.append(vec)
        valids.append(ok)
        gaps.append(jnp.where(ok, reward - vec, 0.0))
    count = sum(lens[r][0:1, 0:1] for r in range(DP))
    mean = sum(jnp.sum(g, axis=1, keepdims=True) for g in gaps) / count
    centered = [jnp.where(ok, g - mean, 0.0) for ok, g in zip(valids, gaps)]
    variance = sum(jnp.sum(c * c, axis=1, keepdims=True) for c in centered) / count
    for r in range(DP):
        small[r : r + 1, :] = values[r]
        small[DP + r : DP + r + 1, :] = jnp.where(
            valids[r], centered[r] * lax.rsqrt(variance + 1e-05), 0.0
        )

    for d in range(1, T):
        fs_send(d).wait_send()
    for i, peer in enumerate(peers):
        mn_send(i, peer).wait_send()
    for d in range(1, S):

        @pl.when(me + d < S)
        def _(d=d):
            for s in range(T):
                kv_send(d, s).wait_send()


def local(
    tokens, attn_gain, w_qkv, w_out, mlp_gain, w_up, w_down, pool_gain, pool_bias, value_weight,
    valid_frames,
):
    T, S, DP = (lax.axis_size("tensor"), lax.axis_size("seq"), lax.axis_size("dp"))
    rows, width = tokens.shape[1:]
    block = rows * T
    fr_dev = block // TOK_FRAME
    chunks = width // LANES
    hcols = w_qkv.shape[2]
    heads = hcols // HEAD_DIM
    assert TOK_FRAME % rows == 0 and S * fr_dev <= LANES
    lens = jnp.broadcast_to(valid_frames.astype(F32)[:, None, None], (DP, chunks, LANES))
    vm = pl.BlockSpec(memory_space=pltpu.VMEM)
    hbm = pl.BlockSpec(memory_space=pl.ANY)
    dma = pltpu.SemaphoreType.DMA
    small_rows = -(-2 * DP // 8) * 8
    hidden, small = pl.pallas_call(
        kernel,
        out_shape=(
            jax.ShapeDtypeStruct((rows, width), BF16),
            jax.ShapeDtypeStruct((small_rows, LANES), F32),
        ),
        in_specs=[vm, vm, hbm, hbm, vm, hbm, hbm, vm, vm, vm, vm],
        out_specs=(vm, vm),
        scratch_shapes=[
            pltpu.VMEM(w_qkv.shape, BF16),
            pltpu.VMEM(w_out.shape, BF16),
            pltpu.VMEM(w_up.shape, BF16),
            pltpu.VMEM(w_down.shape, BF16),
            pltpu.VMEM((T, rows, width), BF16),
            pltpu.VMEM((T, rows, width), BF16),
            pltpu.VMEM((T, rows, hcols), BF16),
            pltpu.VMEM((S, T, 2, rows, hcols), BF16),
            pltpu.VMEM((heads, block, 1), F32),
            pltpu.VMEM((heads, block, 1), F32),
            pltpu.VMEM((heads, block, HEAD_DIM), F32),
            pltpu.VMEM((block, hcols), BF16),
            pltpu.VMEM((T, rows, width), BF16),
            pltpu.VMEM((2, T, rows, width), BF16),
            pltpu.VMEM((rows, width), F32),
            pltpu.VMEM((rows, w_up.shape[1]), BF16),
            pltpu.VMEM((T, chunks, LANES), F32),
            pltpu.VMEM((DP, S, fr_dev, chunks, LANES), F32),
            dma((4,)),
            dma((2, 2, T)),
            dma((2, T)),
            dma((S, T)),
            dma((S, T)),
            dma((2, 2, T)),
            dma((2, 2, T)),
            dma((T,)),
            dma((T,)),
            dma((DP * S,)),
            dma((DP, S)),
        ],
        compiler_params=pltpu.CompilerParams(
            collective_id=0, has_side_effects=True, vmem_limit_bytes=67043328
        ),
    )(
        tokens[0],
        attn_gain[None],
        w_qkv,
        w_out,
        mlp_gain[None],
        w_up,
        w_down,
        pool_gain.reshape(chunks, LANES),
        pool_bias.reshape(chunks, LANES),
        value_weight.reshape(chunks, LANES),
        lens,
    )
    roll, seq = (lax.axis_index("dp"), lax.axis_index("seq"))
    values = lax.dynamic_slice(small, (roll, seq * fr_dev), (1, fr_dev))
    advantages = lax.dynamic_slice(small, (DP + roll, seq * fr_dev), (1, fr_dev))
    return (hidden[None], values, advantages)


def solution(mesh):
    in_specs = (
        P("dp", ("seq", "tensor"), None),
        P(),
        P(None, None, "tensor"),
        P("tensor", None),
        P(),
        P(None, "tensor"),
        P("tensor", None),
        P(),
        P(),
        P(),
        P(),
    )
    out_specs = (P("dp", ("seq", "tensor"), None), P("dp", "seq"), P("dp", "seq"))
    return jax.shard_map(local, mesh=mesh, in_specs=in_specs, out_specs=out_specs, check_vma=False)
```

time: 370 us -> 211 us (0.57)
  waiting for transfers between devices: 230 us -> 0 us
  Pallas kernels: 0 us -> 206 us
  blocking collectives: 46.6 us -> 0 us
  matrix products: 41.7 us -> 0 us
  other arithmetic: 25.7 us -> 0.66 us
  between operations: 16.5 us -> 0.65 us
  local copies, waits for them, and re-layouts: 8.01 us -> 3.91 us
    pallas_call x0 -> x1, Pallas kernels: none -> 206 us  [local(): pl.pallas_call(kernel, out_shape=(jax.ShapeDtypeStruct((rows, width), BF1...]
    all_gather x3 -> x0, waiting for transfers between devices: 102 us -> none  [the longest x1 50 us: local(): block_tokens = lax.all_gather(rows, 'tensor', axis=0, tiled=True)]
    psum x1 -> x0, waiting for transfers between devices: 86 us -> none  [local(): lax.psum(jnp.dot(mixed, w_out, preferred_element_type=jnp.float32).astype...]
    dot_general x6 -> x0, matrix products: 41.7 us -> none  [the longest x1 16.6 us: local(): jnp.dot(up, w_down, preferred_element_type=jnp.float32).astype(jnp.bfloat16)]
    reduce_scatter x1 -> x0, waiting for transfers between devices: 40.9 us -> none  [local(): lax.psum_scatter(jnp.dot(up, w_down, preferred_element_type=jnp.float32)....]
    psum x2 -> x0, blocking collectives: 30.6 us -> none  [the longest x1 17.2 us: local(): sums = lax.psum(sums, 'tensor')]
    reduce_sum x7 -> x0, other arithmetic: 16.1 us -> none  [the longest x2 6.62 us: rms_norm(): square = jnp.mean(floats * floats, axis=-1, keepdims=True)]
    all_gather x2 -> x0, blocking collectives: 16 us -> none  [entering_2(): pieces = jax.tree.map(lambda part: lax.all_gather(part, axis), value)]
  transfers between devices with their start and end apart: 5 -> 0, of which waited for: 5 -> 0; matrix products, arithmetic and copies ran while one was open for 4% -> 0% of each run, Pallas kernels for 0% -> 0%
where the time goes in v1:
time: 211 us
  Pallas kernels  206 us (98%)
  local copies, waits for them, and re-layouts  3.91 us (2%)
    pallas_call x1, Pallas kernels, local(): pl.pallas_call(kernel, out_shape=(jax.ShapeDtypeStruct((rows, width), BF1...  206 us

profile of v1, /device:TPU:0, one launch (start us, length us, event | category | flops | bytes accessed | tf_op | source)
XLA Modules:
  0.0 211.1 jit_solution(2365325132819991279)
XLA Ops:
  0.6 0.7 convert_element_type.3
  1.3 0.7 broadcast_in_dim.17.lens
  2.0 205.9 %shard_map.130 = (bf16[128,2048]{1,0:T(8,128)(2,1)}, f32[8,128]{1,0:T(8,128)}) custom-call(bf16[128,2048]{1,0:T(8,128)(2,1)} %bitcast.8, f32[1,2048]{1,0:T(1,128)} %bitcast.9, bf16[3,2048,512]{2,1,0:T(8,128)(2,1)} %w_qkv_h.1, bf16[512,2048]{1,0:T(8,128)(2,1)} %w_out_h.1, f32[1,2048]{1,0:T(1,128)} %bitcast.10, bf16[2048,2048]{1,0:T(8,128)(2,1)} %w_up_h.1, ...), custom_call_target="tpu_custom_call" | custom-call | tf_op jit(solution)/shard_map/pallas_call | solution.py:389
  207.8 1.4 fusion
  209.2 1.9 copy.15

commit v2 on v1

--- a/solution.py
+++ b/solution.py
@@ -69,24 +69,25 @@
             device_id={"tensor": to}, device_id_type=MESH,
         )
 
-    def gather(buf, which, process):
+    def gather(buf, which, first, size, process):
         def send(s, way):
+            ref = buf.at[s, pl.ds(first, size)]
             return zcopy(
-                buf.at[s], buf.at[s], ag_s.at[which, way, s], ag_r.at[which, s],
-                right if way == 0 else left,
+                ref, ref, ag_s.at[which, way, s], ag_r.at[which, s], right if way == 0 else left
             )
 
-        @pl.when(z < T - 1)
-        def _():
-            send(z, 0).start()
-
-        @pl.when(z > 0)
-        def _():
-            send(z, 1).start()
-
-        process(z)
-
-        def step(k, carry):
+        def begin():
+            @pl.when(z < T - 1)
+            def _():
+                send(z, 0).start()
+
+            @pl.when(z > 0)
+            def _():
+                send(z, 1).start()
+
+            process(z)
+
+        def step(k):
             a, b = (z - k, z + k)
 
             @pl.when(a >= 0)
@@ -113,71 +114,89 @@
             def _():
                 process(b)
 
+        def drain():
+            for s in range(T):
+
+                @pl.when((s <= z) & (z < T - 1))
+                def _():
+                    send(s, 0).wait_send()
+
+                @pl.when((s >= z) & (z > 0))
+                def _():
+                    send(s, 1).wait_send()
+
+        return (begin, step, drain)
+
+    def run_gather(begin, step, drain):
+        begin()
+
+        def body(k, carry):
+            step(k)
             return carry
 
-        lax.fori_loop(1, T, step, 0)
-
-        for s in range(T):
-
-            @pl.when((s <= z) & (z < T - 1))
-            def _():
-                send(s, 0).wait_send()
-
-            @pl.when((s >= z) & (z > 0))
-            def _():
-                send(s, 1).wait_send()
-
-    def scatter(buf, which):
+        lax.fori_loop(1, T, body, 0)
+        drain()
+
+    def scatter(buf, which, first, size):
+        span = pl.ds(first, size)
+
         def send(d, way):
+            ref = buf.at[way, d, span]
             return zcopy(
-                buf.at[way, d], buf.at[way, d], rs_s.at[which, way, d], rs_r.at[which, way, d],
+                ref, ref, rs_s.at[which, way, d], rs_r.at[which, way, d],
                 right if way == 0 else left,
             )
 
-        def hop(d, way, first):
-            @pl.when(first)
-            def _():
-                buf[way, d] = part[d]
-
-            @pl.when(jnp.logical_not(first))
+        def move(d, way, opens):
+            @pl.when(opens)
+            def _():
+                buf[way, d, span] = part[d, span]
+
+            @pl.when(jnp.logical_not(opens))
             def _():
                 send(d, way).wait_recv()
-                buf[way, d] = (buf[way, d].astype(F32) + part[d].astype(F32)).astype(BF16)
+                buf[way, d, span] = (
+                    buf[way, d, span].astype(F32) + part[d, span].astype(F32)
+                ).astype(BF16)
 
             send(d, way).start()
 
-        for k in range(T - 1):
+        def hop(k):
             d = T - 1 - k
 
             @pl.when(z < d)
-            def _(d=d):
-                hop(d, 0, z == 0)
+            def _():
+                move(d, 0, z == 0)
 
             @pl.when(z > k)
-            def _(d=k):
-                hop(d, 1, z == T - 1)
-
-        after[...] = after[...] + part[z].astype(F32)
-
-        @pl.when(z > 0)
-        def _():
-            send(z, 0).wait_recv()
-            after[...] = after[...] + buf[0, z].astype(F32)
-
-        @pl.when(z < T - 1)
-        def _():
-            send(z, 1).wait_recv()
-            after[...] = after[...] + buf[1, z].astype(F32)
-
-        for d in range(T):
-
-            @pl.when(z < d)
-            def _(d=d):
-                send(d, 0).wait_send()
-
-            @pl.when(z > d)
-            def _(d=d):
-                send(d, 1).wait_send()
+            def _():
+                move(k, 1, z == T - 1)
+
+        def finish():
+            after[span] = after[span] + part[z, span].astype(F32)
+
+            @pl.when(z > 0)
+            def _():
+                send(z, 0).wait_recv()
+                after[span] = after[span] + buf[0, z, span].astype(F32)
+
+            @pl.when(z < T - 1)
+            def _():
+                send(z, 1).wait_recv()
+                after[span] = after[span] + buf[1, z, span].astype(F32)
+
+        def drain():
+            for d in range(T):
+
+                @pl.when(z < d)
+                def _(d=d):
+                    send(d, 0).wait_send()
+
+                @pl.when(z > d)
+                def _(d=d):
+                    send(d, 1).wait_send()
+
+        return (hop, finish, drain)
 
     def kv_send(d, s):
         return pltpu.make_async_remote_copy(
@@ -198,7 +217,7 @@
         query[s] = jnp.dot(x, w_qkv[0], preferred_element_type=F32).astype(BF16)
 
     loads[0].wait()
-    gather(ag1, 0, project)
+    run_gather(*gather(ag1, 0, 0, rows, project))
 
     peak[...] = jnp.full_like(peak, -1e30)
     total[...] = jnp.zeros_like(total)
@@ -259,10 +278,6 @@
 
     lax.fori_loop(0, width // tile, out_tile, 0)
     after[...] = tok[...].astype(F32)
-    scatter(rs, 0)
-    rounded = after[...].astype(BF16).astype(F32)
-    after[...] = rounded
-    ag2[z] = rms_norm(rounded, mlp_gain[...])
     loads[2].wait()
     loads[3].wait()
 
@@ -283,8 +298,38 @@
 
         lax.fori_loop(0, width // tile, down_tile, 0)
 
-    gather(ag2, 1, feed)
-    scatter(rs, 1)
+    half = rows // 2
+    hop0, finish0, drain0 = scatter(rs, 0, 0, half)
+    hop1, finish1, drain1 = scatter(rs, 1, half, half)
+    begin0, step0, settle0 = gather(ag2, 1, 0, half, lambda s: None)
+
+    def renorm(first):
+        span = pl.ds(first, half)
+        rounded = after[span].astype(BF16).astype(F32)
+        after[span] = rounded
+        ag2[z, span] = rms_norm(rounded, mlp_gain[...])
+
+    for k in range(T - 1):
+        hop0(k)
+    hop1(0)
+    finish0()
+    renorm(0)
+    begin0()
+    for k in range(1, T):
+        if k < T - 1:
+            hop1(k)
+        step0(k)
+    finish1()
+    drain0()
+    drain1()
+    renorm(half)
+    run_gather(*gather(ag2, 2, half, half, feed))
+    settle0()
+    hop2, finish2, drain2 = scatter(rs, 2, 0, rows)
+    for k in range(T - 1):
+        hop2(k)
+    finish2()
+    drain2()
     out = after[...].astype(BF16)
     hidden[...] = out
     sums = jnp.sum(out.astype(F32), axis=0, keepdims=True)
@@ -414,12 +459,12 @@
             pltpu.VMEM((T, chunks, LANES), F32),
             pltpu.VMEM((DP, S, fr_dev, chunks, LANES), F32),
             dma((4,)),
-            dma((2, 2, T)),
-            dma((2, T)),
+            dma((3, 2, T)),
+            dma((3, T)),
             dma((S, T)),
             dma((S, T)),
-            dma((2, 2, T)),
-            dma((2, 2, T)),
+            dma((3, 2, T)),
+            dma((3, 2, T)),
             dma((T,)),
             dma((T,)),
             dma((DP * S,)),

time: 211 us -> 211 us (level)
  no operation moved by 1% of the time
where the time goes in v2:
time: 211 us; the launch traced here: 210 us
  Pallas kernels  205 us (97%)
  local copies, waits for them, and re-layouts  3.91 us (2%)
    pallas_call x1, Pallas kernels, local(): pl.pallas_call(kernel, out_shape=(jax.ShapeDtypeStruct((rows, width), BF1...  205 us

profile of v2, /device:TPU:0, one launch (start us, length us, event | category | flops | bytes accessed | tf_op | source)
XLA Modules:
  0.0 210.4 jit_solution(8107530327618281792)
XLA Ops:
  0.6 0.7 convert_element_type.3
  1.3 0.7 broadcast_in_dim.17.lens
  2.0 205.2 %shard_map.130 = (bf16[128,2048]{1,0:T(8,128)(2,1)}, f32[8,128]{1,0:T(8,128)}) custom-call(bf16[128,2048]{1,0:T(8,128)(2,1)} %bitcast.8, f32[1,2048]{1,0:T(1,128)} %bitcast.9, bf16[3,2048,512]{2,1,0:T(8,128)(2,1)} %w_qkv_h.1, bf16[512,2048]{1,0:T(8,128)(2,1)} %w_out_h.1, f32[1,2048]{1,0:T(1,128)} %bitcast.10, bf16[2048,2048]{1,0:T(8,128)(2,1)} %w_up_h.1, ...), custom_call_target="tpu_custom_call" | custom-call | tf_op jit(solution)/shard_map/pallas_call | solution.py:434
  207.2 1.4 fusion
  208.5 1.9 copy.15
